TPU v7x, 32 devices: a whole 2x2x4 slice. The times are simulated.
32 devices in a mesh: ta: 2 (over core), gx: 16 (over z, y, x).
Axes of the slice: x: 2, y: 2, z: 4, core: 2. Of those that a mesh axis runs over, the one named last changes fastest.
Arguments:
- time_links: float32 [6, 2, 3, 3, 96, 4608], P('ta', None, None, None, 'gx'), may hold values from -1 to 1, as said below
Outputs:
- loop_planes: float32 [96, 2, 4608], P('gx', None, 'ta')
- correlator: float32 [96, 49], P('gx')
Inputs may be any that keep to these rules, and one draw needn't show every extreme that they name: At every site and time, the matrix time_links[t, 0] + i time_links[t, 1] is special unitary.
All inputs are finite; a program needn't handle non-finite values.
Results may differ from a plain program's by a relative error of at most 0.00029.
Values sent between devices are 32-bit elements; how exact they have to be, the bound alone decides.
A program may use at most 64 MiB of HBM per device.

v0:
```python
import jax
import jax.numpy as jnp
from jax import lax
from jax.sharding import PartitionSpec as P


def prefix(value, axis, join, neutral):
    count, mine = (lax.axis_size(axis), lax.axis_index(axis))
    pieces = lax.all_gather(value, axis)
    subtotal = jnp.full_like(value, 0) + jnp.asarray(neutral, value.dtype)

    def step(position, subtotal):
        longer = join(subtotal, pieces[position])
        return jnp.where(position < mine, longer, subtotal)

    return lax.fori_loop(0, count - 1, step, subtotal)


def spread(value, axis, source):
    kept = jnp.where(lax.axis_index(axis) == source, value, 0).astype(value.dtype)
    return lax.psum(kept, axis)


def complex_mul(left, right):
    terms_real = []
    terms_imag = []
    for middle in range(3):
        left_real = left[0][:, middle : middle + 1]
        left_imag = left[1][:, middle : middle + 1]
        right_real = right[0][middle : middle + 1]
        right_imag = right[1][middle : middle + 1]
        terms_real.append(left_real * right_real - left_imag * right_imag)
        terms_imag.append(left_real * right_imag + left_imag * right_real)
    return jnp.stack(
        [
            terms_real[0] + terms_real[1] + terms_real[2],
            terms_imag[0] + terms_imag[1] + terms_imag[2],
        ]
    )


def trace_third(matrix):
    return (matrix[:, 0, 0] + matrix[:, 1, 1] + matrix[:, 2, 2]) / 3.0


def correlation(own_rows, others):
    return lax.dot_general(
        own_rows,
        others,
        (((1,), (1,)), ((), ())),
        precision=lax.Precision.HIGHEST,
        preferred_element_type=jnp.float32,
    )


def by_separation(products, offset, longest, period):
    row_index = lax.broadcasted_iota(jnp.int32, products.shape, 0)
    column_index = lax.broadcasted_iota(jnp.int32, products.shape, 1)
    separation = offset + column_index - row_index
    separation = separation % period
    targets = jnp.arange(longest + 1, dtype=jnp.int32)
    selector = (separation[:, :, None] == targets).astype(jnp.float32)
    return jnp.sum(products[:, :, None] * selector, axis=1)


def per_device(time_links):
    local_product = time_links[0]
    for slice_index in range(1, time_links.shape[0]):
        local_product = complex_mul(local_product, time_links[slice_index])
    plane_sites = time_links.shape[-1]
    ta_count = lax.axis_size("ta")
    site_share = plane_sites // ta_count
    unit_matrix = jnp.broadcast_to(
        jnp.eye(3, dtype=jnp.float32)[:, :, None, None], local_product.shape[1:]
    )
    identity = jnp.stack([unit_matrix, jnp.zeros_like(unit_matrix)])
    earlier = prefix(local_product, "ta", complex_mul, identity)
    full_product = complex_mul(earlier, local_product)
    traces = spread(trace_third(full_product), "ta", ta_count - 1)
    own_share = lax.dynamic_slice_in_dim(traces, lax.axis_index("ta") * site_share, site_share, 2)
    loop_planes = jnp.transpose(own_share, (1, 0, 2))
    planes = loop_planes.shape[0]
    flat_width = loop_planes.shape[1] * loop_planes.shape[2]
    gx_count = lax.axis_size("gx")
    far_blocks = gx_count // 2
    longest = planes * far_blocks
    own_rows = loop_planes.reshape(planes, flat_width)
    shard_rows = lax.all_gather(loop_planes, "gx", axis=0, tiled=True)
    products = correlation(own_rows, shard_rows.reshape(shard_rows.shape[0], flat_width))
    totals_part = by_separation(
        products, -lax.axis_index("gx") * planes, longest, planes * gx_count
    )
    correlator = lax.psum(totals_part, "ta") / plane_sites
    return (loop_planes, correlator)


def solution(mesh):
    in_specs = (P("ta", None, None, None, "gx", None),)
    out_specs = (P("gx", None, "ta"), P("gx", None))
    return jax.shard_map(
        per_device, mesh=mesh, in_specs=in_specs, out_specs=out_specs, check_vma=False
    )
```

profile of v0, /device:TPU:0, one launch (start us, length us, event | category | flops | bytes accessed | tf_op | source)
XLA Modules:
  0.0 143.7 jit_solution(14677089066934302279)
XLA Ops:
  7.2 5.7 %fusion.13 = (f32[1,1,1,3,6,4608]{5,1,4,3,2,0:T(1,128)S(1)}, f32[1,1,1,3,6,4608]{5,1,4,3,2,0:T(1,128)S(1)}, f32[1,1,1,3,6,4608]{5,1,4,3,2,0:T(1,128)S(1)}, f32[1...) fusion(f32[3,2,3,3,6,4608]{5,1,4,3,2,0:T(2,128)} %param.1), kind=kLoop, calls=%fused_computation.88 | loop fusion | bytes 7962624 | tf_op jit(solution)/shard_map/slice | solution.py:30
  12.9 3.9 %fusion.14 = (f32[1,1,3,3,6,4608]{5,1,4,3,2,0:T(1,128)S(1)}, f32[1,1,3,3,6,4608]{5,1,4,3,2,0:T(1,128)S(1)}) fusion(f32[3,2,3,3,6,4608]{5,1,4,3,2,0:T(2,128)} %param.1), kind=kLoop, calls=%fused_computation.89 | loop fusion | bytes 3981312 | tf_op jit(solution)/shard_map/slice | solution.py:28
  16.9 0.3 copy_bitcast_fusion
  17.8 1.0 subtract_add_fusion.4
  19.3 0.3 copy-done.1
  20.1 0.9 subtract_add_fusion.3
  21.0 1.8 %pad_maximum_fusion = f32[2,3,3,6,4608]{4,3,2,1,0:T(8,128)} fusion(f32[1,3,3,6,4608]{4,3,2,1,0:T(8,128)S(1)} %get-tuple-element.56, f32[1,3,3,6,4608]{4,3,2,1,0:T(8,128)S(1)} %get-tuple-element.55), kind=kLoop, calls=%fused_computation | loop fusion | flops 497664 | bytes 3981312 | tf_op jit(solution)/shard_map/stack | solution.py:34
  22.8 0.2 all-reduce.3.cloned.1.call-start
  23.1 2.4 %subtract_add_fusion.1 = (f32[3,3,6,4608]{3,2,1,0:T(8,128)S(1)}, f32[3,3,6,4608]{3,2,1,0:T(8,128)S(1)}) fusion(f32[3,6,4608]{2,1,0:T(8,128)S(1)} %get-tuple-element.90, f32[3,6,4608]{2,1,0:T(8,128)S(1)} %get-tuple-element.77, f32[3,6,4608]{2,1,0:T(8,128)S(1)} %get-tuple-element.91, f32[3,6,4608]{2,1,0:T(8,128)} %copy-done.3, ...), kind=kLoop, calls=%fused_computation.11 | loop fusion | flops 5474304 | bytes 5971968 | tf_op jit(solution)/shard_map/add | solution.py:36
  25.7 15.4 %all-gather.6.cloned.1.call-done = f32[4,3,3,6,4608]{4,3,2,1,0:T(8,128)} async-done(((f32[2,3,3,6,4608]{4,3,2,1,0:T(8,128)}), f32[4,3,3,6,4608]{4,3,2,1,0:T(8,128)}) %all-gather.6.cloned.1.call-update) | async-done | bytes 3981328 | tf_op jit(solution)/shard_map/all_gather | solution.py:9
  41.0 2.1 %broadcast_multiply_fusion.5 = (f32[3,6,4608]{2,1,0:T(8,128)S(1)}, f32[3,6,4608]{2,1,0:T(8,128)S(1)}, f32[3,6,4608]{2,1,0:T(8,128)S(1)}, f32[3,6,4608]{2,1,0:T(8...) fusion(f32[2,2,3,3,6,4608]{5,4,3,2,1,0:T(8,128)} %bitcast.118), kind=kLoop, calls=%fused_computation.72 | loop fusion | flops 497664 | bytes 3981312 | tf_op jit(solution)/shard_map/while/body/eval_jaxpr/mul | solution.py:32
  43.1 1.2 copy-done
  44.3 0.2 slice_bitcast_fusion.19
  44.5 0.9 subtract_add_fusion.2
  45.5 0.3 maximum_select_fusion
  46.3 1.0 subtract_add_fusion
  47.2 0.8 fusion.8
  48.1 19.6 %all-reduce.3.cloned.1.call-done = f32[2,6,4608]{2,1,0:T(8,128)} async-done(((f32[2,6,4608]{2,1,0:T(8,128)}), f32[2,6,4608]{2,1,0:T(8,128)}) %all-reduce.3.cloned.1.call-update) | async-done | bytes 221200 | tf_op jit(solution)/shard_map/psum | solution.py:21
  67.7 0.9 dynamic-slice_bitcast_fusion
  68.6 0.7 copy.52
  69.3 61.6 %all-gather.4.cloned.1.call-done = f32[96,2,2304]{2,1,0:T(2,128)} async-done(((f32[6,2,2304]{2,1,0:T(2,128)}), f32[96,2,2304]{2,1,0:T(2,128)}) %all-gather.4.cloned.1.call-update) | async-done | bytes 1769488 | tf_op jit(solution)/shard_map/all_gather | solution.py:88
  131.0 2.9 %fusion.2 = f32[6,96]{1,0:T(8,128)S(1)} fusion(f32[6,2,2304]{2,0,1:T(8,128)S(1)} %dynamic-slice_bitcast_fusion, f32[96,2,2304]{2,1,0:T(2,128)} %all-gather.4.cloned.1.call-done), kind=kOutput, calls=%fused_computation.18 | convolution fusion | flops 31850496 | bytes 1882368 | tf_op jit(solution)/shard_map/dot_general | solution.py:47
  134.1 2.5 %psum.15 = f32[6,49]{1,0:T(8,128)S(1)} all-reduce(f32[6,49]{1,0:T(8,128)S(1)} %select_reduce_fusion), channel_id=1, replica_groups=mesh['ta'=2,'gx'=16] {'ta'}, use_global_device_ids=true, to_apply=%region_2.3 | all-reduce | flops 294 | bytes 2352 | tf_op jit(solution)/shard_map/psum | solution.py:93
  136.5 0.6 broadcast_multiply_fusion.6
  (34 shorter events, 2.5 us)
Async XLA Ops:
  7.2 33.9 %all-gather.6.cloned.1.call-start = ((), (), s32[]{:S(2)}) async-start(), calls=%async_computation.2 | async-start | bytes 7962624 | tf_op jit(solution)/shard_map/all_gather | solution.py:9
  18.8 0.8 copy-start.1
  18.9 0.8 copy-start.2
  18.9 1.0 copy-start.3
  19.0 1.1 copy-start.4
  22.8 44.8 %all-reduce.3.cloned.1.call-start = ((), (), s32[]{:S(2)}) async-start(), calls=%async_computation | async-start | bytes 589824 | tf_op jit(solution)/shard_map/psum | solution.py:21
  41.0 3.3 %copy-start = (f32[4,3,3,6,4608]{4,3,2,1,0:T(8,128)S(1)}, f32[4,3,3,6,4608]{4,3,2,1,0:T(8,128)}, u32[]{:S(2)}) copy-start(f32[4,3,3,6,4608]{4,3,2,1,0:T(8,128)} %all-gather.6.cloned.1.call-done) | copy-start | bytes 11943940
  48.0 82.9 %all-gather.4.cloned.1.call-start = ((), (), s32[]{:S(2)}) async-start(), calls=%async_computation.1 | async-start | bytes 1880064 | tf_op jit(solution)/shard_map/all_gather | solution.py:88
Sparse Core Ops, SparseCore 0:
  22.9 18.0 all-gather.5
  48.2 19.4 all-reduce.2
  71.0 59.8 all-gather.3
where the time goes:
time: 144 us
  waiting for transfers between devices  96.6 us (67%)
  local copies, waits for them, and re-layouts  15.5 us (11%)
  between operations  14 us (10%)
  other arithmetic  11.8 us (8%)
  matrix products  2.94 us (2%)
  blocking collectives  2.47 us (2%)
    all_gather x1, waiting for transfers between devices, per_device(): shard_rows = lax.all_gather(loop_planes, 'gx', axis=0, tiled=True)  61.6 us
    psum x1, waiting for transfers between devices, spread(): return lax.psum(kept, axis)  19.6 us
    all_gather x1, waiting for transfers between devices, prefix(): pieces = lax.all_gather(value, axis)  15.4 us
    add x5, other arithmetic, complex_mul(): terms_real[0] + terms_real[1] + terms_real[2]  6.09 us
    slice x1, local copies, waits for them, and re-layouts, complex_mul(): right_real = right[0][middle:middle + 1]  5.72 us
    slice x2, local copies, waits for them, and re-layouts, complex_mul(): left_real = left[0][:, middle:middle + 1]  3.92 us
    dot_general x1, matrix products, correlation(): lax.dot_general(own_rows, others, (((1,), (1,)), ((), ())), precision=lax...  2.94 us
  transfers between devices with their start and end apart: 3, of which 3 were waited for; matrix products, arithmetic and copies ran while one was open for 2% of the time, Pallas kernels for 0%

commit v1 on v0

--- a/solution.py
+++ b/solution.py
@@ -18,7 +18,7 @@
 
 def spread(value, axis, source):
     kept = jnp.where(lax.axis_index(axis) == source, value, 0).astype(value.dtype)
-    return lax.psum(kept, axis)
+    return jnp.sum(lax.all_gather(kept, axis), axis=0)
 
 
 def complex_mul(left, right):

time: 144 us -> 126 us (0.88)
  waiting for transfers between devices: 96.6 us -> 68.4 us
  local copies, waits for them, and re-layouts: 15.5 us -> 20.6 us
  other arithmetic: 11.8 us -> 14.6 us
  blocking collectives: 2.47 us -> 4.6 us
    psum x1 -> x0, waiting for transfers between devices: 19.6 us -> none  [spread(): return lax.psum(kept, axis)]
    all_gather x1, waiting for transfers between devices: 15.4 us -> 8.38 us  [prefix(): pieces = lax.all_gather(value, axis)]
    mul x15 -> x21, local copies, waits for them, and re-layouts: 1.6 us -> 7.12 us  [complex_mul(): terms_real.append(left_real * right_real - left_imag * right_imag)]
    add x5, other arithmetic: 6.09 us -> 8.55 us  [complex_mul(): terms_real[0] + terms_real[1] + terms_real[2]]
    all_gather x0 -> x1, blocking collectives: none -> 2.12 us  [spread(): return jnp.sum(lax.all_gather(kept, axis), axis=0)]
    all_gather x1, waiting for transfers between devices: 61.6 us -> 60 us  [per_device(): shard_rows = lax.all_gather(loop_planes, 'gx', axis=0, tiled=True)]
  transfers between devices with their start and end apart: 3 -> 2, of which waited for: 3 -> 2; matrix products, arithmetic and copies ran while one was open for 2% -> 8% of each run, Pallas kernels for 0% -> 0%
where the time goes in v1:
time: 126 us
  waiting for transfers between devices  68.4 us (54%)
  local copies, waits for them, and re-layouts  20.6 us (16%)
  other arithmetic  14.6 us (12%)
  between operations  14.4 us (11%)
  blocking collectives  4.6 us (4%)
  matrix products  2.94 us (2%)
    all_gather x1, waiting for transfers between devices, per_device(): shard_rows = lax.all_gather(loop_planes, 'gx', axis=0, tiled=True)  60 us
    add x5, other arithmetic, complex_mul(): terms_real[0] + terms_real[1] + terms_real[2]  8.55 us
    all_gather x1, waiting for transfers between devices, prefix(): pieces = lax.all_gather(value, axis)  8.38 us
    mul x21, local copies, waits for them, and re-layouts, complex_mul(): terms_real.append(left_real * right_real - left_imag * right_imag)  7.12 us
    slice x1, local copies, waits for them, and re-layouts, complex_mul(): right_real = right[0][middle:middle + 1]  5.72 us
    slice x2, local copies, waits for them, and re-layouts, complex_mul(): left_real = left[0][:, middle:middle + 1]  3.92 us
    dot_general x1, matrix products, correlation(): lax.dot_general(own_rows, others, (((1,), (1,)), ((), ())), precision=lax...  2.94 us
    unnamed x20, local copies, waits for them, and re-layouts  2.68 us
  transfers between devices with their start and end apart: 2, of which 2 were waited for; matrix products, arithmetic and copies ran while one was open for 8% of the time, Pallas kernels for 0%

profile of v1, /device:TPU:0, one launch (start us, length us, event | category | flops | bytes accessed | tf_op | source)
XLA Modules:
  0.0 125.8 jit_solution(3021290334226141167)
XLA Ops:
  7.2 5.7 %fusion.10 = (f32[1,1,1,3,6,4608]{5,1,4,3,2,0:T(1,128)S(1)}, f32[1,1,1,3,6,4608]{5,1,4,3,2,0:T(1,128)S(1)}, f32[1,1,1,3,6,4608]{5,1,4,3,2,0:T(1,128)S(1)}, f32[1...) fusion(f32[3,2,3,3,6,4608]{5,1,4,3,2,0:T(2,128)} %param.1), kind=kLoop, calls=%fused_computation.87 | loop fusion | bytes 7962624 | tf_op jit(solution)/shard_map/slice | solution.py:30
  12.9 3.9 %fusion.11 = (f32[1,1,3,3,6,4608]{5,1,4,3,2,0:T(1,128)S(1)}, f32[1,1,3,3,6,4608]{5,1,4,3,2,0:T(1,128)S(1)}) fusion(f32[3,2,3,3,6,4608]{5,1,4,3,2,0:T(2,128)} %param.1), kind=kLoop, calls=%fused_computation.88 | loop fusion | bytes 3981312 | tf_op jit(solution)/shard_map/slice | solution.py:28
  17.8 1.0 subtract_add_fusion.4
  20.1 0.9 subtract_add_fusion.3
  21.0 1.8 %pad_maximum_fusion = f32[2,3,3,6,4608]{4,3,2,1,0:T(8,128)} fusion(f32[1,3,3,6,4608]{4,3,2,1,0:T(8,128)S(1)} %get-tuple-element.60, f32[1,3,3,6,4608]{4,3,2,1,0:T(8,128)S(1)} %get-tuple-element.59), kind=kLoop, calls=%fused_computation | loop fusion | flops 497664 | bytes 3981312 | tf_op jit(solution)/shard_map/stack | solution.py:34
  23.1 1.0 copy.110
  24.1 1.0 copy.109
  25.1 1.0 copy.108
  26.1 1.0 copy.107
  27.1 1.0 copy.106
  28.4 3.8 %subtract_add_fusion.1 = (f32[3,3,6,4608]{3,1,2,0:T(4,128)S(1)}, f32[3,3,6,4608]{3,1,2,0:T(4,128)S(1)}) fusion(f32[3,6,4608]{2,0,1:T(4,128)} %copy.110, f32[3,6,4608]{2,1,0:T(8,128)S(1)} %get-tuple-element.81, f32[3,6,4608]{2,0,1:T(4,128)} %copy.109, f32[3,6,4608]{2,1,0:T(8,128)S(1)} %copy-done.6, f32[3,6,4608]{2,0,1:T(4,128)} %copy.108, ...), kind=kLoop, calls=%fused_computation.11 | loop fusion | flops 5474304 | bytes 5971968 | tf_op jit(solution)/shard_map/add | solution.py:36
  32.6 8.4 %all-gather.7.cloned.1.call-done = f32[4,3,3,6,4608]{4,3,2,1,0:T(8,128)} async-done(((f32[2,3,3,6,4608]{4,3,2,1,0:T(8,128)}), f32[4,3,3,6,4608]{4,3,2,1,0:T(8,128)}) %all-gather.7.cloned.1.call-update) | async-done | bytes 3981328 | tf_op jit(solution)/shard_map/all_gather | solution.py:9
  41.0 2.1 %broadcast_multiply_fusion.5 = (f32[3,6,4608]{2,1,0:T(8,128)S(1)}, f32[3,6,4608]{2,1,0:T(8,128)S(1)}, f32[3,6,4608]{2,1,0:T(8,128)S(1)}, f32[3,6,4608]{2,1,0:T(8...) fusion(f32[2,2,3,3,6,4608]{5,4,3,2,1,0:T(8,128)} %bitcast.119), kind=kLoop, calls=%fused_computation.70 | loop fusion | flops 497664 | bytes 3981312 | tf_op jit(solution)/shard_map/while/body/eval_jaxpr/mul | solution.py:32
  43.1 1.2 copy-done
  44.5 0.9 subtract_add_fusion.2
  46.3 2.0 %subtract_add_fusion = (f32[1,3,3,6,4608]{4,2,3,1,0:T(4,128)S(1)}, f32[1,3,3,6,4608]{4,2,3,1,0:T(4,128)S(1)}) fusion(f32[3,6,4608]{2,0,1:T(4,128)S(1)} %get-tuple-element.75, f32[3,6,4608]{2,1,0:T(8,128)S(1)} %get-tuple-element.72, f32[3,6,4608]{2,0,1:T(4,128)S(1)} %get-tuple-element.69, f32[3,6,4608]{2,1,0:T(8,128)S(1)} %get-tuple-element.66, ...), kind=kLoop, calls=%fused_computation.9 | loop fusion | flops 5474304 | bytes 5971968 | tf_op jit(solution)/shard_map/add | solution.py:36
  48.3 0.7 broadcast_select_fusion
  49.0 2.1 %all-gather.1 = f32[4,1,1,6,4608]{4,2,3,1,0:T(1,128)S(1)} all-gather(f32[2,1,1,6,4608]{4,2,3,1,0:T(1,128)S(1)} %broadcast_select_fusion), channel_id=3, replica_groups=mesh['ta'=2,'gx'=16] {'ta'}, dimensions={0}, use_global_device_ids=true | all-gather | bytes 663552 | tf_op jit(solution)/shard_map/all_gather | solution.py:21
  51.3 0.3 reshape.307
  52.0 0.7 copy.115
  52.8 60.0 %all-gather.5.cloned.1.call-done = f32[96,2,2304]{2,1,0:T(2,128)} async-done(((f32[6,2,2304]{2,1,0:T(2,128)}), f32[96,2,2304]{2,1,0:T(2,128)}) %all-gather.5.cloned.1.call-update) | async-done | bytes 1769488 | tf_op jit(solution)/shard_map/all_gather | solution.py:88
  112.8 2.9 %fusion.2 = f32[6,96]{1,0:T(8,128)S(1)} fusion(f32[96,2,2304]{2,1,0:T(2,128)} %all-gather.5.cloned.1.call-done, f32[2,6,2304]{2,0,1:T(2,128)S(1)} %constant_dynamic-slice_fusion), kind=kOutput, calls=%fused_computation.18 | convolution fusion | flops 31850496 | bytes 1882368 | tf_op jit(solution)/shard_map/dot_general | solution.py:47
  115.8 2.5 %psum.7 = f32[6,49]{1,0:T(8,128)S(1)} all-reduce(f32[6,49]{1,0:T(8,128)S(1)} %select_reduce_fusion), channel_id=1, replica_groups=mesh['ta'=2,'gx'=16] {'ta'}, use_global_device_ids=true, to_apply=%region_2.3 | all-reduce | flops 294 | bytes 2352 | tf_op jit(solution)/shard_map/psum | solution.py:93
  118.3 0.6 broadcast_multiply_fusion.6
  (50 shorter events, 4.8 us)
Async XLA Ops:
  7.2 33.8 %all-gather.7.cloned.1.call-start = ((), (), s32[]{:S(2)}) async-start(), calls=%async_computation.1 | async-start | bytes 7962624 | tf_op jit(solution)/shard_map/all_gather | solution.py:9
  18.8 0.8 copy-start.1
  18.9 0.8 copy-start.3
  18.9 1.0 copy-start.5
  19.0 1.1 copy-start.7
  22.8 89.9 %all-gather.5.cloned.1.call-start = ((), (), s32[]{:S(2)}) async-start(), calls=%async_computation | async-start | bytes 1880064 | tf_op jit(solution)/shard_map/all_gather | solution.py:88
  26.1 2.3 %copy-start.2 = (f32[3,6,4608]{2,1,0:T(8,128)S(1)}, f32[3,6,4608]{2,1,0:T(8,128)}, u32[]{:S(2)}) copy-start(f32[3,6,4608]{2,1,0:T(8,128)} %copy-done.1) | copy-start | bytes 995332
  26.1 2.3 %copy-start.4 = (f32[3,6,4608]{2,1,0:T(8,128)S(1)}, f32[3,6,4608]{2,1,0:T(8,128)}, u32[]{:S(2)}) copy-start(f32[3,6,4608]{2,1,0:T(8,128)} %copy-done.3) | copy-start | bytes 995332
  26.1 2.3 %copy-start.6 = (f32[3,6,4608]{2,1,0:T(8,128)S(1)}, f32[3,6,4608]{2,1,0:T(8,128)}, u32[]{:S(2)}) copy-start(f32[3,6,4608]{2,1,0:T(8,128)} %copy-done.5) | copy-start | bytes 995332
  27.1 1.3 %copy-start.8 = (f32[3,6,4608]{2,1,0:T(8,128)S(1)}, f32[3,6,4608]{2,1,0:T(8,128)}, u32[]{:S(2)}) copy-start(f32[3,6,4608]{2,1,0:T(8,128)} %copy-done.7) | copy-start | bytes 995332
  41.0 3.3 %copy-start = (f32[4,3,3,6,4608]{4,3,2,1,0:T(8,128)S(1)}, f32[4,3,3,6,4608]{4,3,2,1,0:T(8,128)}, u32[]{:S(2)}) copy-start(f32[4,3,3,6,4608]{4,3,2,1,0:T(8,128)} %all-gather.7.cloned.1.call-done) | copy-start | bytes 11943940
Sparse Core Ops, SparseCore 0:
  22.9 18.0 all-gather.6
  52.8 59.8 all-gather.4
